TPU v7x, 128 devices: a whole 4x4x4 slice. The times are simulated.
128 devices in a mesh: row: 8 (over z_hi, y), col: 8 (over x, core), mp: 2 (over z_lo).
Axes of the slice: x: 4, y: 4, z: 4 (z_hi: 2, z_lo: 2; z = z_hi * 2 + z_lo), core: 2. Of those that a mesh axis runs over, the one named last changes fastest.
Arguments:
- weights: bfloat16 [8, 8, 5, 2304, 1024], P('row', 'col', None, None, 'mp'), may hold values from -6 to 6
- warm_down: bfloat16 [8, 8, 5, 4, 1024], P('row', 'col', None, None, 'mp'), may hold values from -6 to 6
- warm_right: bfloat16 [8, 8, 5, 4, 1024], P('row', 'col', None, None, 'mp'), may hold values from -6 to 6
Outputs:
- new_weights: bfloat16 [8, 8, 5, 2304, 1024], P('row', 'col', None, None, 'mp')
- next_down: float32 [8, 8, 5, 4, 1024], P('row', 'col', None, None, 'mp')
- next_right: float32 [8, 8, 5, 4, 1024], P('row', 'col', None, None, 'mp')
All inputs are finite; a program needn't handle non-finite values.
Results may differ from a plain program's by a relative error of at most 0.0085.
Values may be sent and summed in bfloat16 or wider, within the bound.
A program may use at most 128 MiB of HBM per device.

v0:
```python
import jax
import jax.numpy as jnp
from jax import lax
from jax.sharding import PartitionSpec as P

ROUNDS = 2


step_size = 0.2
epsilon = 1e-06


def passed_along(value, axis, by):
    devices = lax.axis_size(axis)
    return lax.ppermute(value, axis, [(i, (i + by) % devices) for i in range(devices)])


def from_everyone(value, axis):
    copies = jnp.broadcast_to(value, (lax.axis_size(axis), *value.shape))
    return lax.all_to_all(copies, axis, split_axis=0, concat_axis=0, tiled=True)


def taken_together(value, axis):
    everything = from_everyone(value, axis)
    return jnp.sum(everything, axis=0)


def orthonormal(vectors):
    basis = []
    for column in range(vectors.shape[-2]):
        source = vectors[..., column, :]
        update = source
        for earlier in basis:
            update = update - jnp.sum(source * earlier, axis=-1, keepdims=True) * earlier
        basis.append(update / jnp.sqrt(jnp.sum(update * update, axis=-1, keepdims=True) + epsilon))
    return jnp.stack(basis, axis=-2)


def neighbours(payload):
    from_above = passed_along(payload[:, 1].astype(jnp.bfloat16), "row", 1).astype(jnp.float32)
    from_below = passed_along(payload[:, 0], "row", -1)
    from_left = passed_along(payload[:, 3].astype(jnp.bfloat16), "col", 1).astype(jnp.float32)
    from_right = passed_along(payload[:, 2].astype(jnp.bfloat16), "col", -1).astype(jnp.float32)
    return jnp.stack([from_above, from_below, from_left, from_right], 1)


def gossip_round(layers, factors):
    partial_rows = jnp.einsum("lerk,ldk->lerd", factors, layers, preferred_element_type=jnp.float32)
    totals = taken_together(partial_rows, "mp")
    difference = totals - neighbours(totals)
    basis = orthonormal(difference).astype(jnp.bfloat16)
    own_back = jnp.einsum("lerd,ldk->lerk", basis, layers, preferred_element_type=jnp.float32)
    combined = own_back + neighbours(own_back)
    next_factors = combined.astype(jnp.bfloat16)
    count_layers = layers.shape[0]
    flat_basis = basis.reshape(count_layers, -1, basis.shape[-1])
    flat_factors = next_factors.reshape(count_layers, -1, next_factors.shape[-1])
    correction = jnp.einsum(
        "lsd,lsk->ldk", flat_basis, flat_factors, preferred_element_type=jnp.float32
    )
    updated = (layers.astype(jnp.float32) - step_size * correction).astype(jnp.bfloat16)
    return (updated, next_factors, combined)


def body(weights, warm_down, warm_right):
    above = passed_along(warm_down, "row", 1)
    beside = passed_along(warm_right, "col", 1)
    layers = weights[0, 0]
    factors = jnp.stack([above[0, 0], warm_down[0, 0], beside[0, 0], warm_right[0, 0]], axis=1)
    combined = jnp.zeros(factors.shape, jnp.float32)
    for repeat in range(ROUNDS):
        layers, factors, combined = gossip_round(layers, factors)
    return (layers[None, None], combined[:, 1][None, None], combined[:, 3][None, None])


def solution(mesh):
    placed = (
        P("row", "col", None, None, "mp"),
        P("row", "col", None, None, "mp"),
        P("row", "col", None, None, "mp"),
    )
    return jax.shard_map(
        body,
        mesh=mesh,
        in_specs=placed,
        out_specs=(
            P("row", "col", None, None, "mp"),
            P("row", "col", None, None, "mp"),
            P("row", "col", None, None, "mp"),
        ),
        check_vma=False,
    )
```

profile of v0, /device:TPU:24, one launch (start us, length us, event | category | flops | bytes accessed | tf_op | source)
XLA Modules:
  0.0 146.0 jit_solution(8086439782705276956)
XLA Ops:
  0.6 3.6 %collective-permute-start = (bf16[1,1,5,4,512]{4,3,2,1,0:T(4,128)(2,1)}, bf16[1,1,5,4,512]{4,3,2,1,0:T(4,128)(2,1)S(1)}, u32[]{:S(2)}, u32[]{:S(2)}) collective-permute-start(bf16[1,1,5,4,512]{4,3,2,1,0:T(4,128)(2,1)} %param.4), channel_id=1, source_target_pairs={{0,16},{16,32},{32,48},{48,64},{64,80},{80,96},{96,112},{112,0},{1... | collective-permute-start | bytes 61448 | tf_op jit(solution)/shard_map/ppermute | solution.py:15
  4.2 1.7 %collective-permute-done = bf16[1,1,5,4,512]{4,3,2,1,0:T(4,128)(2,1)S(1)} collective-permute-done((bf16[1,1,5,4,512]{4,3,2,1,0:T(4,128)(2,1)}, bf16[1,1,5,4,512]{4,3,2,1,0:T(4,128)(2,1)S(1)}, u32[]{:S(2)}, u32[]{:S(2)}) %collective-permute-start) | collective-permute-done | bytes 20512 | tf_op jit(solution)/shard_map/ppermute | solution.py:15
  5.9 2.9 %collective-permute-done.1 = bf16[1,1,5,4,512]{4,3,2,1,0:T(4,128)(2,1)S(1)} collective-permute-done((bf16[1,1,5,4,512]{4,3,2,1,0:T(4,128)(2,1)}, bf16[1,1,5,4,512]{4,3,2,1,0:T(4,128)(2,1)S(1)}, u32[]{:S(2)}, u32[]{:S(2)}) %collective-permute-start.1) | collective-permute-done | bytes 20512 | tf_op jit(solution)/shard_map/ppermute | solution.py:15
  8.9 7.6 %fusion.6 = f32[5,4,4,2304]{3,2,1,0:T(4,128)S(1)} fusion(bf16[1,1,5,2304,512]{4,3,2,1,0:T(8,128)(2,1)} %param.3, bf16[5,1,4,512]{3,2,1,0:T(4,128)(2,1)} %bitcast.289, bf16[5,1,4,512]{3,2,1,0:T(4,128)(2,1)S(1)} %bitcast.292, bf16[5,1,4,512]{3,2,1,0:T(4,128)(2,1)} %bitcast.290, bf16[5,1,4,512]{3,2,1,0:T(4,128)(2,1)S(1)} %bitcast.291), kind=kOutput, calls=%fused_computation.8 | convolution fusion | flops 189071360 | bytes 12615680 | tf_op jit(solution)/shard_map/lerk,ldk->lerd/dot_general | solution.py:48
  16.7 19.2 %all_to_all.10 = f32[2,5,4,4,2304]{4,3,2,1,0:T(4,128)S(1)} all-to-all(f32[2,5,4,4,2304]{4,3,2,1,0:T(4,128)S(1)} %broadcast_in_dim.6), channel_id=1, replica_groups=mesh['row'=8,'col'=8,'mp'=2] {'mp'}, dimensions={0} | all-to-all | bytes 2949120 | tf_op jit(solution)/shard_map/all_to_all | solution.py:20
  36.8 3.6 %collective-permute-start.2 = (bf16[5,4,2304]{2,1,0:T(4,128)(2,1)S(1)}, bf16[5,4,2304]{2,1,0:T(4,128)(2,1)S(1)}, u32[]{:S(2)}, u32[]{:S(2)}) collective-permute-start(bf16[5,4,2304]{2,1,0:T(4,128)(2,1)S(1)} %get-tuple-element.38), channel_id=1, source_target_pairs={{0,16},{16,32},{32,48},{48,64},{64,80},{80,96},{96,112},{112,0},{1... | collective-permute-start | bytes 276488 | tf_op jit(solution)/shard_map/ppermute | solution.py:15
  41.1 1.5 %collective-permute-done.2 = bf16[5,4,2304]{2,1,0:T(4,128)(2,1)S(1)} collective-permute-done((bf16[5,4,2304]{2,1,0:T(4,128)(2,1)S(1)}, bf16[5,4,2304]{2,1,0:T(4,128)(2,1)S(1)}, u32[]{:S(2)}, u32[]{:S(2)}) %collective-permute-start.2) | collective-permute-done | bytes 92192 | tf_op jit(solution)/shard_map/ppermute | solution.py:15
  42.7 3.0 %collective-permute-done.4 = bf16[5,4,2304]{2,1,0:T(4,128)(2,1)S(1)} collective-permute-done((bf16[5,4,2304]{2,1,0:T(4,128)(2,1)S(1)}, bf16[5,4,2304]{2,1,0:T(4,128)(2,1)S(1)}, u32[]{:S(2)}, u32[]{:S(2)}) %collective-permute-start.4) | collective-permute-done | bytes 92192 | tf_op jit(solution)/shard_map/ppermute | solution.py:15
  46.4 3.3 %collective-permute-done.3 = f32[5,4,2304]{2,1,0:T(4,128)S(1)} collective-permute-done((f32[5,4,2304]{2,1,0:T(4,128)S(1)}, f32[5,4,2304]{2,1,0:T(4,128)S(1)}, u32[]{:S(2)}, u32[]{:S(2)}) %collective-permute-start.3) | collective-permute-done | bytes 184352 | tf_op jit(solution)/shard_map/ppermute | solution.py:15
  52.8 6.3 %fusion.4 = f32[5,4,4,512]{3,1,2,0:T(4,128)S(1)} fusion(bf16[1,1,5,2304,512]{4,3,2,1,0:T(8,128)(2,1)} %param.3, bf16[5,4,1,2304]{3,1,2,0:T(4,128)(2,1)S(1)} %get-tuple-element.28, bf16[5,4,1,2304]{3,1,2,0:T(4,128)(2,1)S(1)} %get-tuple-element.29, bf16[5,4,1,2304]{3,1,2,0:T(4,128)(2,1)S(1)} %get-tuple-element.30, ...), kind=kOutput, calls=%fused_computation.6 | convolution fusion | flops 190218240 | bytes 12328960 | tf_op jit(solution)/shard_map/lerd,ldk->lerk/dot_general | solution.py:52
  59.8 2.4 %collective-permute-start.6 = (bf16[5,4,512]{2,1,0:T(4,128)(2,1)S(1)}, bf16[5,4,512]{2,1,0:T(4,128)(2,1)S(1)}, u32[]{:S(2)}, u32[]{:S(2)}) collective-permute-start(bf16[5,4,512]{2,1,0:T(4,128)(2,1)S(1)} %get-tuple-element.46), channel_id=1, source_target_pairs={{0,16},{16,32},{32,48},{48,64},{64,80},{80,96},{96,112},{112,0},{1... | collective-permute-start | bytes 61448 | tf_op jit(solution)/shard_map/ppermute | solution.py:15
  63.7 2.9 %collective-permute-done.8 = bf16[5,4,512]{2,1,0:T(4,128)(2,1)S(1)} collective-permute-done((bf16[5,4,512]{2,1,0:T(4,128)(2,1)S(1)}, bf16[5,4,512]{2,1,0:T(4,128)(2,1)S(1)}, u32[]{:S(2)}, u32[]{:S(2)}) %collective-permute-start.8) | collective-permute-done | bytes 20512 | tf_op jit(solution)/shard_map/ppermute | solution.py:15
  66.8 3.6 %collective-permute-done.7 = f32[5,4,512]{2,1,0:T(4,128)S(1)} collective-permute-done((f32[5,4,512]{2,1,0:T(4,128)S(1)}, f32[5,4,512]{2,1,0:T(4,128)S(1)}, u32[]{:S(2)}, u32[]{:S(2)}) %collective-permute-start.7) | collective-permute-done | bytes 40992 | tf_op jit(solution)/shard_map/ppermute | solution.py:15
  70.6 8.9 %subtract_convert_fusion.1 = bf16[5,2304,512]{2,1,0:T(8,128)(2,1)} fusion(bf16[5,16,2304]{2,1,0:T(8,128)(2,1)S(1)} %convert_element_type.97, bf16[5,16,512]{2,1,0:T(8,128)(2,1)S(1)} %reshape.90, bf16[1,1,5,2304,512]{4,3,2,1,0:T(8,128)(2,1)} %param.3), kind=kOutput, calls=%fused_computation.1 | convolution fusion | flops 212336640 | bytes 24043520 | tf_op jit(solution)/shard_map/lsd,lsk->ldk/dot_general | solution.py:58
  79.6 7.6 %fusion.2 = f32[5,4,4,2304]{3,2,1,0:T(4,128)S(1)} fusion(bf16[5,2304,512]{2,1,0:T(8,128)(2,1)} %subtract_convert_fusion.1, bf16[5,4,4,512]{3,1,2,0:T(4,128)(2,1)S(1)} %fusion.45), kind=kOutput, calls=%fused_computation.4 | convolution fusion | flops 188743680 | bytes 12615680 | tf_op jit(solution)/shard_map/lerk,ldk->lerd/dot_general | solution.py:48
  87.4 19.9 %all_to_all.11 = f32[2,5,4,4,2304]{4,3,2,1,0:T(4,128)S(1)} all-to-all(f32[2,5,4,4,2304]{4,3,2,1,0:T(4,128)S(1)} %broadcast_in_dim.7), channel_id=1, replica_groups=mesh['row'=8,'col'=8,'mp'=2] {'mp'}, dimensions={0} | all-to-all | bytes 2949120 | tf_op jit(solution)/shard_map/all_to_all | solution.py:20
  108.4 2.1 %collective-permute-start.11 = (f32[5,4,2304]{2,1,0:T(4,128)S(1)}, f32[5,4,2304]{2,1,0:T(4,128)S(1)}, u32[]{:S(2)}, u32[]{:S(2)}) collective-permute-start(f32[5,4,2304]{2,1,0:T(4,128)S(1)} %slice_bitcast_fusion), channel_id=1, source_target_pairs={{0,112},{16,0},{32,16},{48,32},{64,48},{80,64},{96,80},{112,96},{1... | collective-permute-start | bytes 552968 | tf_op jit(solution)/shard_map/ppermute | solution.py:15
  110.4 1.3 collective-permute-start.13
  113.9 3.0 %collective-permute-done.12 = bf16[5,4,2304]{2,1,0:T(4,128)(2,1)S(1)} collective-permute-done((bf16[5,4,2304]{2,1,0:T(4,128)(2,1)S(1)}, bf16[5,4,2304]{2,1,0:T(4,128)(2,1)S(1)}, u32[]{:S(2)}, u32[]{:S(2)}) %collective-permute-start.12) | collective-permute-done | bytes 92192 | tf_op jit(solution)/shard_map/ppermute | solution.py:15
  120.7 1.9 %fusion = f32[5,4,4,512]{3,1,2,0:T(4,128)S(1)} fusion(bf16[5,2304,512]{2,1,0:T(8,128)(2,1)S(1)} %copy-done, bf16[5,4,1,2304]{3,1,2,0:T(4,128)(2,1)S(1)} %get-tuple-element.21, bf16[5,4,1,2304]{3,1,2,0:T(4,128)(2,1)S(1)} %get-tuple-element.22, bf16[5,4,1,2304]{3,1,2,0:T(4,128)(2,1)S(1)} %get-tuple-element.23, bf16[5,4,1,2304]{3,1,2,0:T(4,128)(2,1)S(1)} %get-tuple-element.24), kind=kOutput, calls=%fused_computation.2 | convolution fusion | flops 190218240 | bytes 12328960 | tf_op jit(solution)/shard_map/lerd,ldk->lerk/dot_general | solution.py:52
  123.4 3.9 %collective-permute-start.14 = (bf16[5,4,512]{2,1,0:T(4,128)(2,1)S(1)}, bf16[5,4,512]{2,1,0:T(4,128)(2,1)S(1)}, u32[]{:S(2)}, u32[]{:S(2)}) collective-permute-start(bf16[5,4,512]{2,1,0:T(4,128)(2,1)S(1)} %get-tuple-element.43), channel_id=1, source_target_pairs={{0,16},{16,32},{32,48},{48,64},{64,80},{80,96},{96,112},{112,0},{1... | collective-permute-start | bytes 61448 | tf_op jit(solution)/shard_map/ppermute | solution.py:15
  128.8 2.9 %collective-permute-done.16 = bf16[5,4,512]{2,1,0:T(4,128)(2,1)S(1)} collective-permute-done((bf16[5,4,512]{2,1,0:T(4,128)(2,1)S(1)}, bf16[5,4,512]{2,1,0:T(4,128)(2,1)S(1)}, u32[]{:S(2)}, u32[]{:S(2)}) %collective-permute-start.16) | collective-permute-done | bytes 20512 | tf_op jit(solution)/shard_map/ppermute | solution.py:15
  131.9 3.6 %collective-permute-done.15 = f32[5,4,512]{2,1,0:T(4,128)S(1)} collective-permute-done((f32[5,4,512]{2,1,0:T(4,128)S(1)}, f32[5,4,512]{2,1,0:T(4,128)S(1)}, u32[]{:S(2)}, u32[]{:S(2)}) %collective-permute-start.15) | collective-permute-done | bytes 40992 | tf_op jit(solution)/shard_map/ppermute | solution.py:15
  137.1 8.9 %fusion.8 = bf16[1,1,5,2304,512]{4,3,2,1,0:T(8,128)(2,1)} fusion(bf16[5,16,2304]{2,1,0:T(8,128)(2,1)S(1)} %convert_element_type.108, bf16[5,16,512]{2,1,0:T(8,128)(2,1)S(1)} %reshape.91, bf16[5,2304,512]{2,1,0:T(8,128)(2,1)} %subtract_convert_fusion.1), kind=kOutput, calls=%fused_computation.10 | convolution fusion | flops 212336640 | bytes 24043520 | tf_op jit(solution)/shard_map/lsd,lsk->ldk/dot_general | solution.py:58
  (107 shorter events, 19.1 us)
Async XLA Ops:
  0.6 5.3 %collective-permute-start = (bf16[1,1,5,4,512]{4,3,2,1,0:T(4,128)(2,1)}, bf16[1,1,5,4,512]{4,3,2,1,0:T(4,128)(2,1)S(1)}, u32[]{:S(2)}, u32[]{:S(2)}) collective-permute-start(bf16[1,1,5,4,512]{4,3,2,1,0:T(4,128)(2,1)} %param.4), channel_id=1, source_target_pairs={{0,16},{16,32},{32,48},{48,64},{64,80},{80,96},{96,112},{112,0},{1... | collective-permute-start | bytes 61448 | tf_op jit(solution)/shard_map/ppermute | solution.py:15
  4.2 4.6 %collective-permute-start.1 = (bf16[1,1,5,4,512]{4,3,2,1,0:T(4,128)(2,1)}, bf16[1,1,5,4,512]{4,3,2,1,0:T(4,128)(2,1)S(1)}, u32[]{:S(2)}, u32[]{:S(2)}) collective-permute-start(bf16[1,1,5,4,512]{4,3,2,1,0:T(4,128)(2,1)} %param.5), channel_id=1, source_target_pairs={{0,2},{2,4},{4,6},{6,8},{8,10},{10,12},{12,14},{14,0},{1,3},{3,5},... | collective-permute-start | bytes 61448 | tf_op jit(solution)/shard_map/ppermute | solution.py:15
  36.8 5.8 %collective-permute-start.2 = (bf16[5,4,2304]{2,1,0:T(4,128)(2,1)S(1)}, bf16[5,4,2304]{2,1,0:T(4,128)(2,1)S(1)}, u32[]{:S(2)}, u32[]{:S(2)}) collective-permute-start(bf16[5,4,2304]{2,1,0:T(4,128)(2,1)S(1)} %get-tuple-element.38), channel_id=1, source_target_pairs={{0,16},{16,32},{32,48},{48,64},{64,80},{80,96},{96,112},{112,0},{1... | collective-permute-start | bytes 276488 | tf_op jit(solution)/shard_map/ppermute | solution.py:15
  40.5 9.2 %collective-permute-start.3 = (f32[5,4,2304]{2,1,0:T(4,128)S(1)}, f32[5,4,2304]{2,1,0:T(4,128)S(1)}, u32[]{:S(2)}, u32[]{:S(2)}) collective-permute-start(f32[5,4,2304]{2,1,0:T(4,128)S(1)} %slice_bitcast_fusion.1), channel_id=1, source_target_pairs={{0,112},{16,0},{32,16},{48,32},{64,48},{80,64},{96,80},{112,96},{1... | collective-permute-start | bytes 552968 | tf_op jit(solution)/shard_map/ppermute | solution.py:15
  40.6 2.2 %collective-permute-start.5 = (bf16[5,4,2304]{2,1,0:T(4,128)(2,1)S(1)}, bf16[5,4,2304]{2,1,0:T(4,128)(2,1)S(1)}, u32[]{:S(2)}, u32[]{:S(2)}) collective-permute-start(bf16[5,4,2304]{2,1,0:T(4,128)(2,1)S(1)} %get-tuple-element.39), channel_id=1, source_target_pairs={{0,14},{2,0},{4,2},{6,4},{8,6},{10,8},{12,10},{14,12},{1,15},{3,1}... | collective-permute-start | bytes 276488 | tf_op jit(solution)/shard_map/ppermute | solution.py:15
  40.6 5.2 %collective-permute-start.4 = (bf16[5,4,2304]{2,1,0:T(4,128)(2,1)S(1)}, bf16[5,4,2304]{2,1,0:T(4,128)(2,1)S(1)}, u32[]{:S(2)}, u32[]{:S(2)}) collective-permute-start(bf16[5,4,2304]{2,1,0:T(4,128)(2,1)S(1)} %get-tuple-element.40), channel_id=1, source_target_pairs={{0,2},{2,4},{4,6},{6,8},{8,10},{10,12},{12,14},{14,0},{1,3},{3,5},... | collective-permute-start | bytes 276488 | tf_op jit(solution)/shard_map/ppermute | solution.py:15
  59.8 3.9 %collective-permute-start.6 = (bf16[5,4,512]{2,1,0:T(4,128)(2,1)S(1)}, bf16[5,4,512]{2,1,0:T(4,128)(2,1)S(1)}, u32[]{:S(2)}, u32[]{:S(2)}) collective-permute-start(bf16[5,4,512]{2,1,0:T(4,128)(2,1)S(1)} %get-tuple-element.46), channel_id=1, source_target_pairs={{0,16},{16,32},{32,48},{48,64},{64,80},{80,96},{96,112},{112,0},{1... | collective-permute-start | bytes 61448 | tf_op jit(solution)/shard_map/ppermute | solution.py:15
  62.2 4.5 %collective-permute-start.9 = (bf16[5,4,512]{2,1,0:T(4,128)(2,1)S(1)}, bf16[5,4,512]{2,1,0:T(4,128)(2,1)S(1)}, u32[]{:S(2)}, u32[]{:S(2)}) collective-permute-start(bf16[5,4,512]{2,1,0:T(4,128)(2,1)S(1)} %get-tuple-element.47), channel_id=1, source_target_pairs={{0,14},{2,0},{4,2},{6,4},{8,6},{10,8},{12,10},{14,12},{1,15},{3,1}... | collective-permute-start | bytes 61448 | tf_op jit(solution)/shard_map/ppermute | solution.py:15
  62.2 4.4 %collective-permute-start.8 = (bf16[5,4,512]{2,1,0:T(4,128)(2,1)S(1)}, bf16[5,4,512]{2,1,0:T(4,128)(2,1)S(1)}, u32[]{:S(2)}, u32[]{:S(2)}) collective-permute-start(bf16[5,4,512]{2,1,0:T(4,128)(2,1)S(1)} %get-tuple-element.48), channel_id=1, source_target_pairs={{0,2},{2,4},{4,6},{6,8},{8,10},{10,12},{12,14},{14,0},{1,3},{3,5},... | collective-permute-start | bytes 61448 | tf_op jit(solution)/shard_map/ppermute | solution.py:15
  62.7 7.6 %collective-permute-start.7 = (f32[5,4,512]{2,1,0:T(4,128)S(1)}, f32[5,4,512]{2,1,0:T(4,128)S(1)}, u32[]{:S(2)}, u32[]{:S(2)}) collective-permute-start(f32[5,4,512]{2,1,0:T(4,128)S(1)} %slice_bitcast_fusion.11), channel_id=1, source_target_pairs={{0,112},{16,0},{32,16},{48,32},{64,48},{80,64},{96,80},{112,96},{1... | collective-permute-start | bytes 122888 | tf_op jit(solution)/shard_map/ppermute | solution.py:15
  108.0 12.7 %copy-start = (bf16[5,2304,512]{2,1,0:T(8,128)(2,1)S(1)}, bf16[5,2304,512]{2,1,0:T(8,128)(2,1)}, u32[]{:S(2)}) copy-start(bf16[5,2304,512]{2,1,0:T(8,128)(2,1)} %subtract_convert_fusion.1) | copy-start | bytes 35389444
  108.3 4.6 %collective-permute-start.10 = (bf16[5,4,2304]{2,1,0:T(4,128)(2,1)S(1)}, bf16[5,4,2304]{2,1,0:T(4,128)(2,1)S(1)}, u32[]{:S(2)}, u32[]{:S(2)}) collective-permute-start(bf16[5,4,2304]{2,1,0:T(4,128)(2,1)S(1)} %get-tuple-element.35), channel_id=1, source_target_pairs={{0,16},{16,32},{32,48},{48,64},{64,80},{80,96},{96,112},{112,0},{1... | collective-permute-start | bytes 276488 | tf_op jit(solution)/shard_map/ppermute | solution.py:15
  108.4 9.2 %collective-permute-start.11 = (f32[5,4,2304]{2,1,0:T(4,128)S(1)}, f32[5,4,2304]{2,1,0:T(4,128)S(1)}, u32[]{:S(2)}, u32[]{:S(2)}) collective-permute-start(f32[5,4,2304]{2,1,0:T(4,128)S(1)} %slice_bitcast_fusion), channel_id=1, source_target_pairs={{0,112},{16,0},{32,16},{48,32},{64,48},{80,64},{96,80},{112,96},{1... | collective-permute-start | bytes 552968 | tf_op jit(solution)/shard_map/ppermute | solution.py:15
  110.4 3.4 %collective-permute-start.13 = (bf16[5,4,2304]{2,1,0:T(4,128)(2,1)S(1)}, bf16[5,4,2304]{2,1,0:T(4,128)(2,1)S(1)}, u32[]{:S(2)}, u32[]{:S(2)}) collective-permute-start(bf16[5,4,2304]{2,1,0:T(4,128)(2,1)S(1)} %get-tuple-element.36), channel_id=1, source_target_pairs={{0,14},{2,0},{4,2},{6,4},{8,6},{10,8},{12,10},{14,12},{1,15},{3,1}... | collective-permute-start | bytes 276488 | tf_op jit(solution)/shard_map/ppermute | solution.py:15
  111.7 5.2 %collective-permute-start.12 = (bf16[5,4,2304]{2,1,0:T(4,128)(2,1)S(1)}, bf16[5,4,2304]{2,1,0:T(4,128)(2,1)S(1)}, u32[]{:S(2)}, u32[]{:S(2)}) collective-permute-start(bf16[5,4,2304]{2,1,0:T(4,128)(2,1)S(1)} %get-tuple-element.37), channel_id=1, source_target_pairs={{0,2},{2,4},{4,6},{6,8},{8,10},{10,12},{12,14},{14,0},{1,3},{3,5},... | collective-permute-start | bytes 276488 | tf_op jit(solution)/shard_map/ppermute | solution.py:15
  123.4 5.4 %collective-permute-start.14 = (bf16[5,4,512]{2,1,0:T(4,128)(2,1)S(1)}, bf16[5,4,512]{2,1,0:T(4,128)(2,1)S(1)}, u32[]{:S(2)}, u32[]{:S(2)}) collective-permute-start(bf16[5,4,512]{2,1,0:T(4,128)(2,1)S(1)} %get-tuple-element.43), channel_id=1, source_target_pairs={{0,16},{16,32},{32,48},{48,64},{64,80},{80,96},{96,112},{112,0},{1... | collective-permute-start | bytes 61448 | tf_op jit(solution)/shard_map/ppermute | solution.py:15
  127.3 4.5 %collective-permute-start.17 = (bf16[5,4,512]{2,1,0:T(4,128)(2,1)S(1)}, bf16[5,4,512]{2,1,0:T(4,128)(2,1)S(1)}, u32[]{:S(2)}, u32[]{:S(2)}) collective-permute-start(bf16[5,4,512]{2,1,0:T(4,128)(2,1)S(1)} %get-tuple-element.44), channel_id=1, source_target_pairs={{0,14},{2,0},{4,2},{6,4},{8,6},{10,8},{12,10},{14,12},{1,15},{3,1}... | collective-permute-start | bytes 61448 | tf_op jit(solution)/shard_map/ppermute | solution.py:15
  127.3 4.4 %collective-permute-start.16 = (bf16[5,4,512]{2,1,0:T(4,128)(2,1)S(1)}, bf16[5,4,512]{2,1,0:T(4,128)(2,1)S(1)}, u32[]{:S(2)}, u32[]{:S(2)}) collective-permute-start(bf16[5,4,512]{2,1,0:T(4,128)(2,1)S(1)} %get-tuple-element.45), channel_id=1, source_target_pairs={{0,2},{2,4},{4,6},{6,8},{8,10},{10,12},{12,14},{14,0},{1,3},{3,5},... | collective-permute-start | bytes 61448 | tf_op jit(solution)/shard_map/ppermute | solution.py:15
  127.8 7.6 %collective-permute-start.15 = (f32[5,4,512]{2,1,0:T(4,128)S(1)}, f32[5,4,512]{2,1,0:T(4,128)S(1)}, u32[]{:S(2)}, u32[]{:S(2)}) collective-permute-start(f32[5,4,512]{2,1,0:T(4,128)S(1)} %slice_bitcast_fusion.10), channel_id=1, source_target_pairs={{0,112},{16,0},{32,16},{48,32},{64,48},{80,64},{96,80},{112,96},{1... | collective-permute-start | bytes 122888 | tf_op jit(solution)/shard_map/ppermute | solution.py:15
where the time goes:
time: 146 us
  matrix products  41.3 us (28%)
  blocking collectives  39.1 us (27%)
  waiting for transfers between devices  32.7 us (22%)
  starting transfers between devices  18.6 us (13%)
  other arithmetic  8.48 us (6%)
  local copies, waits for them, and re-layouts  4.71 us (3%)
    all_to_all x2, blocking collectives, from_everyone(): return lax.all_to_all(copies, axis, split_axis=0, concat_axis=0, tiled=True)  39.1 us
    ppermute x18, waiting for transfers between devices, passed_along(): lax.ppermute(value, axis, [(i, (i + by) % devices) for i in range(devices)])  32.7 us
    ppermute x18, starting transfers between devices, passed_along(): lax.ppermute(value, axis, [(i, (i + by) % devices) for i in range(devices)])  18.6 us
    dot_general x2, matrix products, gossip_round(): jnp.einsum('lsd,lsk->ldk', flat_basis, flat_factors, preferred_element_ty...  17.9 us
    dot_general x2, matrix products, gossip_round(): jnp.einsum('lerk,ldk->lerd', factors, layers, preferred_element_type=jnp....  15.2 us
    dot_general x2, matrix products, gossip_round(): jnp.einsum('lerd,ldk->lerk', basis, layers, preferred_element_type=jnp.fl...  8.21 us
  transfers between devices with their start and end apart: 18, of which 16 were waited for; matrix products, arithmetic and copies ran while one was open for 1% of the time, Pallas kernels for 0%

commit v1 on v0

v1 whole, which is shorter than its diff:
```python
import functools

import jax
import jax.numpy as jnp
from jax import lax
from jax.experimental import pallas as pl
from jax.experimental.pallas import tpu as pltpu
from jax.sharding import PartitionSpec as P

STEP = 0.2
EPS = 1e-06
MESH = pl.DeviceIdType.MESH
F32, BF16 = jnp.float32, jnp.bfloat16
NT = (((1,), (1,)), ((), ()))
NN = (((1,), (0,)), ((), ()))
TN = (((0,), (0,)), ((), ()))


def low_half(shape):
    return lax.broadcasted_iota(jnp.int32, shape, len(shape) - 2) % 8 < 4


def dot(a, b, dims):
    return lax.dot_general(a, b, dims, preferred_element_type=F32)


def orthonormal(total, others, chunks):
    sums = [None] * 4
    for j in range(chunks):
        v = total(j) - others(j)
        for s in range(4):
            term = v * (pltpu.roll(v, s, 1) if s else v)
            sums[s] = term if sums[s] is None else sums[s] + term
    gram = []
    for s in range(4):
        g = jnp.broadcast_to(jnp.sum(sums[s], axis=-1, keepdims=True), sums[s].shape)
        gram.append(g + pltpu.roll(g, 4, 1))

    def at(i, j):
        g = gram[i - j]
        return pltpu.roll(g, 8 - i, 1) if i else g

    g = [[at(i, j) for j in range(i + 1)] for i in range(4)]
    c = [[lax.rsqrt(g[0][0] + EPS)]]
    for k in range(1, 4):
        along = [sum(c[j][i] * g[k][i] for i in range(j + 1)) for j in range(k)]
        m = [-sum(along[j] * c[j][i] for j in range(i, k)) for i in range(k)]
        square = g[k][k]
        for i in range(k):
            inner = 2.0 * g[k][i] + m[i] * g[i][i]
            for j in range(i):
                inner = inner + 2.0 * (m[j] * g[i][j])
            square = square + m[i] * inner
        norm = lax.rsqrt(jnp.maximum(square, 0.0) + EPS)
        c.append([norm * x for x in m] + [norm])
    row = lax.broadcasted_iota(jnp.int32, g[0][0].shape, 1) % 4
    columns = []
    for s in range(4):
        column = jnp.zeros(g[0][0].shape, F32)
        for k in range(s, 4):
            value = c[k][k - s]
            column = jnp.where(row == k, pltpu.roll(value, k, 1) if k else value, column)
        columns.append(column)
    out = []
    for j in range(chunks):
        v = total(j) - others(j)
        p = columns[0] * v
        for s in range(1, 4):
            p = p + columns[s] * pltpu.roll(v, s, 1)
        out.append(p)
    return out


def exchange_kernel(
    w_hbm, wd_hbm, wr_hbm, p_ref, f_ref, cd_ref, cr_ref,
    w, warm, total, send1, recv1, send2, recv2, back, send3, recv3,
    w_sem, warm_sem, warm_send, warm_recv, s1, r1, s2, r2, s3, r3,
):
    layers, depth, width = w.shape
    half = depth // 2
    chunks = half // 128
    row, col, mp = lax.axis_index("row"), lax.axis_index("col"), lax.axis_index("mp")
    down, up = lax.rem(row + 1, 8), lax.rem(row + 7, 8)
    right, left = lax.rem(col + 1, 8), lax.rem(col + 7, 8)
    cross_down = lax.rem(mp + lax.div(lax.rem(row, 4), 3), 2)
    cross_up = lax.rem(mp + lax.div(lax.rem(row + 3, 4), 3), 2)
    partner = (row, col, 1 - mp)
    straight = [(down, col, mp), (row, right, mp), (up, col, mp), (row, left, mp)]
    crossed = [(down, col, cross_down), (row, right, mp), (up, col, cross_up), (row, left, mp)]

    barrier = pltpu.get_barrier_semaphore()
    for device in [partner] + straight + [crossed[0], crossed[2]]:
        pl.semaphore_signal(barrier, inc=1, device_id=device, device_id_type=MESH)

    def warm_load(e):
        return pltpu.make_async_copy([wd_hbm, wr_hbm][e].at[0, 0], warm.at[e], warm_sem.at[e])

    def w_load(l):
        return pltpu.make_async_copy(w_hbm.at[0, 0, l], w.at[l], w_sem.at[l])

    for e in range(2):
        warm_load(e).start()
    for l in range(layers):
        w_load(l).start()

    def warm_copy(e):
        return pltpu.make_async_remote_copy(
            warm.at[e], warm.at[e + 2], warm_send.at[e], warm_recv.at[e], device_id=straight[e], device_id_type=MESH)

    def mp_copy(r, l, e, n):
        return pltpu.make_async_remote_copy(
            send1.at[r, l, pl.ds(e, n)], recv1.at[r, l, pl.ds(e, n)], s1.at[r, l, e // 2], r1.at[r, l, e // 2],
            device_id=partner, device_id_type=MESH)

    def sum_copy(r, l, e):
        return pltpu.make_async_remote_copy(
            send2.at[r, l, e], recv2.at[r, l, (e + 2) % 4], s2.at[r, l], r2.at[r, l],
            device_id=crossed[e], device_id_type=MESH)

    def sums_copy(r, l):
        return pltpu.make_async_remote_copy(
            send2.at[r, l], recv2.at[r, l], s2.at[r, l], r2.at[r, l], device_id=partner, device_id_type=MESH)

    def back_copy(r, l, e):
        return pltpu.make_async_remote_copy(
            send3.at[r, l, e], recv3.at[r, l, (e + 2) % 4], s3.at[r, l], r3.at[r, l],
            device_id=straight[e], device_id_type=MESH)

    def backs_copy(r, l):
        return pltpu.make_async_remote_copy(
            send3.at[r, l], recv3.at[r, l], s3.at[r, l], r3.at[r, l], device_id=partner, device_id_type=MESH)

    def forward(factors, l):
        first = dot(factors, w[l, :half], NT)
        second = dot(factors, w[l, half:], NT)
        return jnp.where(low_half(first.shape), first, second)

    def first_forward(l, e):
        pieces = []
        for i in (e, e + 1):
            rows = warm[i, l].astype(F32)
            pieces += [rows, rows]
        product = forward(jnp.concatenate(pieces, axis=0).astype(BF16), l)
        product = product.reshape(2, 8, half)
        total[l, e:e + 2] = product
        send1[0, l, e:e + 2] = product.astype(BF16)
        mp_copy(0, l, e, 2).start()

    def own_edges(l, _):
        w_load(l).wait()
        first_forward(l, 0)

    def other_edges(l, _):
        first_forward(l, 2)

    def add_up(r, l, e, n):
        mp_copy(r, l, e, n).wait_recv()
        value = total[l, e:e + n] + recv1[r, l, e:e + n].astype(F32)
        total[l, e:e + n] = value
        send2[r, l, e:e + n] = value.astype(BF16)
        for i in range(e, e + n):
            sum_copy(r, l, i).start()

    def backward(r, l):
        sums_copy(r, l).wait_recv()

        def mine(j):
            return total[l, :, :, 128 * j:128 * (j + 1)]

        def theirs(j):
            return recv2[r, l, :, :, 128 * j:128 * (j + 1)].astype(F32)

        for j, piece in enumerate(orthonormal(mine, theirs, chunks)):
            p_ref[l, 32 * r:32 * (r + 1), 128 * j:128 * (j + 1)] = piece.reshape(32, 128).astype(BF16)
        basis = p_ref[l, 32 * r:32 * (r + 1)]
        first = dot(basis, w[l, :half], NN)
        second = dot(basis, w[l, half:], NN)
        parts = jnp.where(low_half(first.shape), first, second)
        if r:
            overlap = dot(basis, p_ref[l, :32], NT)
            same = low_half(overlap.shape) == (lax.broadcasted_iota(jnp.int32, overlap.shape, 1) % 8 < 4)
            overlap = jnp.where(same, overlap, 0.0).astype(BF16)
            parts = parts - STEP * dot(overlap, f_ref[l, :32], NN)
        parts = parts.reshape(4, 8, width)
        value = parts + pltpu.roll(parts, 4, 1)
        back[l] = value
        send3[r, l] = value.astype(BF16)
        for e in range(4):
            back_copy(r, l, e).start()

    def combine(r, l):
        backs_copy(r, l).wait_recv()
        value = back[l] + recv3[r, l].astype(F32)
        factors = value.reshape(32, width).astype(BF16)
        f_ref[l, 32 * r:32 * (r + 1)] = factors
        return value, factors

    def second_forward(l, _):
        _, factors = combine(0, l)
        product = forward(factors, l)
        overlap = dot(factors, factors, NT)
        same = low_half(overlap.shape) == (lax.broadcasted_iota(jnp.int32, overlap.shape, 1) % 8 < 4)
        overlap = jnp.where(same, overlap, 0.0).astype(BF16)
        product = product - STEP * dot(overlap, p_ref[l, :32], NN)
        product = product.reshape(4, 8, half)
        total[l] = product
        send1[1, l] = product.astype(BF16)
        mp_copy(1, l, 0, 4).start()

    def last(l, _):
        value, _ = combine(1, l)
        cd_ref[l] = value[0, :4]
        cr_ref[l] = value[1, :4]

    def each(function):
        lax.fori_loop(0, layers, lambda l, carry: (function(l, None), carry)[1], 0)

    for e in range(2):
        warm_load(e).wait()
    pl.semaphore_wait(barrier, 7)
    for e in range(2):
        warm_copy(e).start()
    each(own_edges)
    for e in range(2):
        warm_copy(e).wait_recv()
    each(other_edges)
    each(lambda l, _: (add_up(0, l, 0, 2), add_up(0, l, 2, 2)))
    each(lambda l, _: backward(0, l))
    each(second_forward)
    each(lambda l, _: add_up(1, l, 0, 4))
    each(lambda l, _: backward(1, l))
    each(last)
    for e in range(2):
        warm_copy(e).wait_send()

    def drain(l, _):
        mp_copy(0, l, 0, 2).wait_send()
        mp_copy(0, l, 2, 2).wait_send()
        mp_copy(1, l, 0, 4).wait_send()
        for r in range(2):
            sums_copy(r, l).wait_send()
            backs_copy(r, l).wait_send()

    each(drain)


def exchange(weights, warm_down, warm_right):
    layers, depth, width = weights.shape[2:]
    half = depth // 2
    vmem = pl.BlockSpec(memory_space=pltpu.VMEM)
    hbm = pl.BlockSpec(memory_space=pltpu.HBM)
    dma = pltpu.SemaphoreType.DMA
    return pl.pallas_call(
        exchange_kernel,
        out_shape=(
            jax.ShapeDtypeStruct((layers, 64, half), BF16),
            jax.ShapeDtypeStruct((layers, 64, width), BF16),
            jax.ShapeDtypeStruct((layers, 4, width), F32),
            jax.ShapeDtypeStruct((layers, 4, width), F32),
        ),
        in_specs=[hbm] * 3,
        out_specs=(vmem,) * 4,
        scratch_shapes=[
            pltpu.VMEM((layers, depth, width), BF16),
            pltpu.VMEM((4, layers, 4, width), BF16),
            pltpu.VMEM((layers, 4, 8, half), F32),
            pltpu.VMEM((2, layers, 4, 8, half), BF16),
            pltpu.VMEM((2, layers, 4, 8, half), BF16),
            pltpu.VMEM((2, layers, 4, 8, half), BF16),
            pltpu.VMEM((2, layers, 4, 8, half), BF16),
            pltpu.VMEM((layers, 4, 8, width), F32),
            pltpu.VMEM((2, layers, 4, 8, width), BF16),
            pltpu.VMEM((2, layers, 4, 8, width), BF16),
            dma((layers,)), dma((2,)), dma((2,)), dma((2,)),
            dma((2, layers, 2)), dma((2, layers, 2)),
            dma((2, layers)), dma((2, layers)), dma((2, layers)), dma((2, layers)),
        ],
        compiler_params=pltpu.CompilerParams(collective_id=0, has_side_effects=True, vmem_limit_bytes=48 * 2**20),
        name="exchange",
    )(weights, warm_down, warm_right)


def update_kernel(w_ref, p_ref, f_ref, cd_ref, cr_ref, out_ref, down_ref, right_ref):
    keep = low_half(f_ref.shape[1:]) == (pl.program_id(1) == 0)
    factors = jnp.where(keep, f_ref[0], jnp.zeros_like(f_ref[0]))
    correction = dot(p_ref[0], factors, TN)
    out_ref[0, 0, 0] = (w_ref[0, 0, 0].astype(F32) - STEP * correction).astype(BF16)
    down_ref[0, 0] = cd_ref[...]
    right_ref[0, 0] = cr_ref[...]


def update(weights, basis, factors, down, right):
    layers, depth, width = weights.shape[2:]
    half = depth // 2
    block = pl.BlockSpec((1, 1, 1, half, width), lambda l, h: (0, 0, l, h, 0))
    whole = pl.BlockSpec((layers, 4, width), lambda l, h: (0, 0, 0))
    placed = pl.BlockSpec((1, 1, layers, 4, width), lambda l, h: (0, 0, 0, 0, 0))
    return pl.pallas_call(
        update_kernel,
        grid=(layers, 2),
        out_shape=(
            jax.ShapeDtypeStruct(weights.shape, BF16),
            jax.ShapeDtypeStruct((1, 1, layers, 4, width), F32),
            jax.ShapeDtypeStruct((1, 1, layers, 4, width), F32),
        ),
        in_specs=[
            block,
            pl.BlockSpec((1, 64, half), lambda l, h: (l, 0, 0)),
            pl.BlockSpec((1, 64, width), lambda l, h: (l, 0, 0)),
            whole,
            whole,
        ],
        out_specs=(block, placed, placed),
        name="update",
    )(weights, basis, factors, down, right)


def body(weights, warm_down, warm_right):
    return update(weights, *exchange(weights, warm_down, warm_right))


def solution(mesh):
    placed = (P("row", "col", None, None, "mp"),) * 3
    return jax.shard_map(body, mesh=mesh, in_specs=placed, out_specs=placed, check_vma=False)
```

time: 146 us -> 63.1 us (0.43)
  the two profiles are of different devices: /device:TPU:24 before, /device:TPU:1 now
where the time goes in v1:
time: 63.1 us; the launch traced here: 62.4 us
  Pallas kernels  57.5 us (91%)
  local copies, waits for them, and re-layouts  4.26 us (7%)
  between operations  0.66 us (1%)
    pallas_call x1, Pallas kernels, exchange(): pl.pallas_call(exchange_kernel, out_shape=(jax.ShapeDtypeStruct((layers,...  43.2 us
    pallas_call x1, Pallas kernels, update(): pl.pallas_call(update_kernel, grid=(layers, 2), out_shape=(jax.ShapeDtype...  14.2 us
    unnamed x12, local copies, waits for them, and re-layouts  4.26 us

profile of v1, /device:TPU:1, one launch (start us, length us, event | category | flops | bytes accessed | tf_op | source)
XLA Modules:
  0.0 62.4 jit_solution(2127618383210965851)
XLA Ops:
  0.6 0.0 copy-start.4
  0.6 0.7 %copy-done.4 = bf16[1,1,5,4,512]{4,3,2,1,0:T(4,128)(2,1)S(1)} copy-done((bf16[1,1,5,4,512]{4,3,2,1,0:T(4,128)(2,1)S(1)}, bf16[1,1,5,4,512]{4,3,2,1,0:T(4,128)(2,1)}, u32[]{:S(2)}) %copy-start.4) | copy-done | bytes 20504
  1.4 0.0 copy-start.5
  1.4 0.7 %copy-done.5 = bf16[1,1,5,4,512]{4,3,2,1,0:T(4,128)(2,1)S(1)} copy-done((bf16[1,1,5,4,512]{4,3,2,1,0:T(4,128)(2,1)S(1)}, bf16[1,1,5,4,512]{4,3,2,1,0:T(4,128)(2,1)}, u32[]{:S(2)}) %copy-start.5) | copy-done | bytes 20504
  2.1 43.2 %exchange.1 = (bf16[5,64,1152]{2,1,0:T(8,128)(2,1)S(1)}, bf16[5,64,512]{2,1,0:T(8,128)(2,1)S(1)}, f32[5,4,512]{2,1,0:T(4,128)S(1)}, f32[5,4,512]{2,1,0:T(4,128)S(1)}) custom-call(bf16[1,1,5,2304,512]{4,3,2,1,0:T(8,128)(2,1)} %w_ref.1, bf16[1,1,5,4,512]{4,3,2,1,0:T(4,128)(2,1)S(1)} %copy-done.4, bf16[1,1,5,4,512]{4,3,2,1,0:T(4,128)(2,1)S(1)} %copy-done.5), custom_call_target="tpu_custom_call" | custom-call | tf_op jit(solution)/shard_map/exchange/pallas_call | solution.py:253
  45.3 0.0 copy-start
  45.3 0.9 %copy-done = bf16[5,64,1152]{2,1,0:T(8,128)(2,1)} copy-done((bf16[5,64,1152]{2,1,0:T(8,128)(2,1)}, bf16[5,64,1152]{2,1,0:T(8,128)(2,1)S(1)}, u32[]{:S(2)}) %copy-start) | copy-done | bytes 737304
  46.2 0.0 copy-start.1
  46.2 0.7 %copy-done.1 = bf16[5,64,512]{2,1,0:T(8,128)(2,1)} copy-done((bf16[5,64,512]{2,1,0:T(8,128)(2,1)}, bf16[5,64,512]{2,1,0:T(8,128)(2,1)S(1)}, u32[]{:S(2)}) %copy-start.1) | copy-done | bytes 327704
  46.9 0.0 copy-start.2
  46.9 0.6 copy-done.2
  47.5 0.0 copy-start.3
  47.5 0.6 copy-done.3
  48.1 14.2 %update.1 = (bf16[1,1,5,2304,512]{4,3,2,1,0:T(8,128)(2,1)}, f32[1,1,5,4,512]{4,3,2,1,0:T(4,128)}, f32[1,1,5,4,512]{4,3,2,1,0:T(4,128)}) custom-call(bf16[1,1,5,2304,512]{4,3,2,1,0:T(8,128)(2,1)} %w_ref.1, bf16[5,64,1152]{2,1,0:T(8,128)(2,1)} %copy-done, bf16[5,64,512]{2,1,0:T(8,128)(2,1)} %copy-done.1, f32[5,4,512]{2,1,0:T(4,128)} %copy-done.2, ...), custom_call_target="tpu_custom_call" | custom-call | tf_op jit(solution)/shard_map/update/pallas_call | solution.py:298
Async XLA Ops:
  0.6 0.7 %copy-start.4 = (bf16[1,1,5,4,512]{4,3,2,1,0:T(4,128)(2,1)S(1)}, bf16[1,1,5,4,512]{4,3,2,1,0:T(4,128)(2,1)}, u32[]{:S(2)}) copy-start(bf16[1,1,5,4,512]{4,3,2,1,0:T(4,128)(2,1)} %wd_hbm.1) | copy-start | bytes 61444
  1.4 0.7 %copy-start.5 = (bf16[1,1,5,4,512]{4,3,2,1,0:T(4,128)(2,1)S(1)}, bf16[1,1,5,4,512]{4,3,2,1,0:T(4,128)(2,1)}, u32[]{:S(2)}) copy-start(bf16[1,1,5,4,512]{4,3,2,1,0:T(4,128)(2,1)} %wr_hbm.1) | copy-start | bytes 61444
  45.3 0.9 %copy-start = (bf16[5,64,1152]{2,1,0:T(8,128)(2,1)}, bf16[5,64,1152]{2,1,0:T(8,128)(2,1)S(1)}, u32[]{:S(2)}) copy-start(bf16[5,64,1152]{2,1,0:T(8,128)(2,1)S(1)} %get-tuple-element.7.p_ref) | copy-start | bytes 2211844
  46.2 0.7 %copy-start.1 = (bf16[5,64,512]{2,1,0:T(8,128)(2,1)}, bf16[5,64,512]{2,1,0:T(8,128)(2,1)S(1)}, u32[]{:S(2)}) copy-start(bf16[5,64,512]{2,1,0:T(8,128)(2,1)S(1)} %get-tuple-element.8.f_ref) | copy-start | bytes 983044
  46.9 0.6 copy-start.2
  47.5 0.6 copy-start.3

commit v2 on v1

--- a/solution.py
+++ b/solution.py
@@ -72,8 +72,8 @@
 
 
 def exchange_kernel(
-    w_hbm, wd_hbm, wr_hbm, p_ref, f_ref, cd_ref, cr_ref,
-    w, warm, total, send1, recv1, send2, recv2, back, send3, recv3,
+    w_hbm, wd_hbm, wr_hbm, w, cd_ref, cr_ref,
+    p_ref, f_ref, warm, total, send1, recv1, send2, recv2, back, send3, recv3,
     w_sem, warm_sem, warm_send, warm_recv, s1, r1, s2, r2, s3, r3,
 ):
     layers, depth, width = w.shape
@@ -211,6 +211,12 @@
         value, _ = combine(1, l)
         cd_ref[l] = value[0, :4]
         cr_ref[l] = value[1, :4]
+        factors = f_ref[l]
+        low = low_half(factors.shape)
+        for h in range(2):
+            kept = jnp.where(low == (h == 0), factors, jnp.zeros_like(factors))
+            rows = pl.ds(half * h, half)
+            w[l, rows] = (w[l, rows].astype(F32) - STEP * dot(p_ref[l], kept, TN)).astype(BF16)
 
     def each(function):
         lax.fori_loop(0, layers, lambda l, carry: (function(l, None), carry)[1], 0)
@@ -253,15 +259,15 @@
     return pl.pallas_call(
         exchange_kernel,
         out_shape=(
-            jax.ShapeDtypeStruct((layers, 64, half), BF16),
-            jax.ShapeDtypeStruct((layers, 64, width), BF16),
+            jax.ShapeDtypeStruct((layers, depth, width), BF16),
             jax.ShapeDtypeStruct((layers, 4, width), F32),
             jax.ShapeDtypeStruct((layers, 4, width), F32),
         ),
         in_specs=[hbm] * 3,
-        out_specs=(vmem,) * 4,
+        out_specs=(vmem,) * 3,
         scratch_shapes=[
-            pltpu.VMEM((layers, depth, width), BF16),
+            pltpu.VMEM((layers, 64, half), BF16),
+            pltpu.VMEM((layers, 64, width), BF16),
             pltpu.VMEM((4, layers, 4, width), BF16),
             pltpu.VMEM((layers, 4, 8, half), F32),
             pltpu.VMEM((2, layers, 4, 8, half), BF16),
@@ -275,48 +281,46 @@
             dma((2, layers, 2)), dma((2, layers, 2)),
             dma((2, layers)), dma((2, layers)), dma((2, layers)), dma((2, layers)),
         ],
-        compiler_params=pltpu.CompilerParams(collective_id=0, has_side_effects=True, vmem_limit_bytes=48 * 2**20),
+        compiler_params=pltpu.CompilerParams(collective_id=0, has_side_effects=True, vmem_limit_bytes=20 * 2**20),
         name="exchange",
     )(weights, warm_down, warm_right)
 
 
-def update_kernel(w_ref, p_ref, f_ref, cd_ref, cr_ref, out_ref, down_ref, right_ref):
-    keep = low_half(f_ref.shape[1:]) == (pl.program_id(1) == 0)
-    factors = jnp.where(keep, f_ref[0], jnp.zeros_like(f_ref[0]))
-    correction = dot(p_ref[0], factors, TN)
-    out_ref[0, 0, 0] = (w_ref[0, 0, 0].astype(F32) - STEP * correction).astype(BF16)
-    down_ref[0, 0] = cd_ref[...]
-    right_ref[0, 0] = cr_ref[...]
-
-
-def update(weights, basis, factors, down, right):
-    layers, depth, width = weights.shape[2:]
-    half = depth // 2
-    block = pl.BlockSpec((1, 1, 1, half, width), lambda l, h: (0, 0, l, h, 0))
-    whole = pl.BlockSpec((layers, 4, width), lambda l, h: (0, 0, 0))
-    placed = pl.BlockSpec((1, 1, layers, 4, width), lambda l, h: (0, 0, 0, 0, 0))
+def write_kernel(w_ref, down_ref, right_ref, w_out, down_out, right_out, sems):
+    layers = w_ref.shape[0]
+    copies = [
+        pltpu.make_async_copy(down_ref, down_out.at[0, 0], sems.at[0]),
+        pltpu.make_async_copy(right_ref, right_out.at[0, 0], sems.at[1]),
+    ]
+    copies += [pltpu.make_async_copy(w_ref.at[l], w_out.at[0, 0, l], sems.at[2 + l]) for l in range(layers)]
+    for copy in copies:
+        copy.start()
+    for copy in copies:
+        copy.wait()
+
+
+def write(w, down, right):
+    layers, depth, width = w.shape
+    vmem = pl.BlockSpec(memory_space=pltpu.VMEM)
+    hbm = pl.BlockSpec(memory_space=pltpu.HBM)
     return pl.pallas_call(
-        update_kernel,
-        grid=(layers, 2),
+        write_kernel,
         out_shape=(
-            jax.ShapeDtypeStruct(weights.shape, BF16),
+            jax.ShapeDtypeStruct((1, 1, layers, depth, width), BF16),
             jax.ShapeDtypeStruct((1, 1, layers, 4, width), F32),
             jax.ShapeDtypeStruct((1, 1, layers, 4, width), F32),
         ),
-        in_specs=[
-            block,
-            pl.BlockSpec((1, 64, half), lambda l, h: (l, 0, 0)),
-            pl.BlockSpec((1, 64, width), lambda l, h: (l, 0, 0)),
-            whole,
-            whole,
-        ],
-        out_specs=(block, placed, placed),
-        name="update",
-    )(weights, basis, factors, down, right)
+        in_specs=[vmem] * 3,
+        out_specs=(hbm,) * 3,
+        scratch_shapes=[pltpu.SemaphoreType.DMA((2 + layers,))],
+        compiler_params=pltpu.CompilerParams(vmem_limit_bytes=2**20),
+        name="write",
+    )(w, down, right)
 
 
 def body(weights, warm_down, warm_right):
-    return update(weights, *exchange(weights, warm_down, warm_right))
+    held = [pltpu.with_memory_space_constraint(x, pltpu.HBM) for x in (weights, warm_down, warm_right)]
+    return write(*exchange(*held))
 
 
 def solution(mesh):

time: 63.1 us -> 51.5 us (0.82)
  Pallas kernels: 57.5 us -> 50.8 us
  local copies, waits for them, and re-layouts: 4.26 us -> 0 us
    pallas_call x1, Pallas kernels: 14.2 us -> 4.47 us  [write(): pl.pallas_call(write_kernel, out_shape=(jax.ShapeDtypeStruct((1, 1, layer...]
    unnamed x12 -> x0, local copies, waits for them, and re-layouts: 4.26 us -> none
    pallas_call x1, Pallas kernels: 43.2 us -> 46.3 us  [exchange(): pl.pallas_call(exchange_kernel, out_shape=(jax.ShapeDtypeStruct((layers,...]
where the time goes in v2:
time: 51.5 us; the launch traced here: 51.4 us
  Pallas kernels  50.8 us (99%)
  between operations  0.64 us (1%)
    pallas_call x1, Pallas kernels, exchange(): pl.pallas_call(exchange_kernel, out_shape=(jax.ShapeDtypeStruct((layers,...  46.3 us
    pallas_call x1, Pallas kernels, write(): pl.pallas_call(write_kernel, out_shape=(jax.ShapeDtypeStruct((1, 1, layer...  4.47 us

profile of v2, /device:TPU:1, one launch (start us, length us, event | category | flops | bytes accessed | tf_op | source)
XLA Modules:
  0.0 51.4 jit_solution(3785412397924946940)
XLA Ops:
  0.6 46.3 %exchange.1 = (bf16[5,2304,512]{2,1,0:T(8,128)(2,1)S(1)}, f32[5,4,512]{2,1,0:T(4,128)S(1)}, f32[5,4,512]{2,1,0:T(4,128)S(1)}) custom-call(bf16[1,1,5,2304,512]{4,3,2,1,0:T(8,128)(2,1)} %w_hbm.1, bf16[1,1,5,4,512]{4,3,2,1,0:T(4,128)(2,1)} %wd_hbm.1, bf16[1,1,5,4,512]{4,3,2,1,0:T(4,128)(2,1)} %wr_hbm.1), custom_call_target="tpu_custom_call" | custom-call | tf_op jit(solution)/shard_map/exchange/pallas_call | solution.py:259
  46.9 4.5 %write.1 = (bf16[1,1,5,2304,512]{4,3,2,1,0:T(8,128)(2,1)}, f32[1,1,5,4,512]{4,3,2,1,0:T(4,128)}, f32[1,1,5,4,512]{4,3,2,1,0:T(4,128)}) custom-call(bf16[5,2304,512]{2,1,0:T(8,128)(2,1)S(1)} %get-tuple-element.6.w_ref, f32[5,4,512]{2,1,0:T(4,128)S(1)} %get-tuple-element.7.down_ref, f32[5,4,512]{2,1,0:T(4,128)S(1)} %get-tuple-element.8.right_ref), custom_call_target="tpu_custom_call" | custom-call | tf_op jit(solution)/shard_map/write/pallas_call | solution.py:306

commit v3 on v2

--- a/solution.py
+++ b/solution.py
@@ -71,9 +71,15 @@
     return out
 
 
+def updated(w, basis, factors, h):
+    low = low_half(factors.shape)
+    kept = jnp.where(low == (h == 0), factors, jnp.zeros_like(factors))
+    return (w.astype(F32) - STEP * dot(basis, kept, TN)).astype(BF16)
+
+
 def exchange_kernel(
-    w_hbm, wd_hbm, wr_hbm, w, cd_ref, cr_ref,
-    p_ref, f_ref, warm, total, send1, recv1, send2, recv2, back, send3, recv3,
+    w_hbm, wd_hbm, wr_hbm, w, p_ref, f_ref, cd_ref, cr_ref,
+    wt, warm, total, send1, recv1, send2, recv2, back, send3, recv3,
     w_sem, warm_sem, warm_send, warm_recv, s1, r1, s2, r2, s3, r3,
 ):
     layers, depth, width = w.shape
@@ -100,7 +106,7 @@
 
     for e in range(2):
         warm_load(e).start()
-    for l in range(layers):
+    for l in range(2):
         w_load(l).start()
 
     def warm_copy(e):
@@ -130,9 +136,13 @@
         return pltpu.make_async_remote_copy(
             send3.at[r, l], recv3.at[r, l], s3.at[r, l], r3.at[r, l], device_id=partner, device_id_type=MESH)
 
-    def forward(factors, l):
-        first = dot(factors, w[l, :half], NT)
-        second = dot(factors, w[l, half:], NT)
+    def forward(factors, l, turned=True):
+        if turned:
+            first = dot(factors, wt[l, :, :half], NN)
+            second = dot(factors, wt[l, :, half:], NN)
+        else:
+            first = dot(factors, w[l, :half], NT)
+            second = dot(factors, w[l, half:], NT)
         return jnp.where(low_half(first.shape), first, second)
 
     def first_forward(l, e):
@@ -140,7 +150,7 @@
         for i in (e, e + 1):
             rows = warm[i, l].astype(F32)
             pieces += [rows, rows]
-        product = forward(jnp.concatenate(pieces, axis=0).astype(BF16), l)
+        product = forward(jnp.concatenate(pieces, axis=0).astype(BF16), l, False)
         product = product.reshape(2, 8, half)
         total[l, e:e + 2] = product
         send1[0, l, e:e + 2] = product.astype(BF16)
@@ -148,6 +158,11 @@
 
     def own_edges(l, _):
         w_load(l).wait()
+
+        @pl.when(l + 2 < layers)
+        def _():
+            w_load(l + 2).start()
+
         first_forward(l, 0)
 
     def other_edges(l, _):
@@ -197,7 +212,7 @@
 
     def second_forward(l, _):
         _, factors = combine(0, l)
-        product = forward(factors, l)
+        product = forward(factors, l, False)
         overlap = dot(factors, factors, NT)
         same = low_half(overlap.shape) == (lax.broadcasted_iota(jnp.int32, overlap.shape, 1) % 8 < 4)
         overlap = jnp.where(same, overlap, 0.0).astype(BF16)
@@ -211,15 +226,18 @@
         value, _ = combine(1, l)
         cd_ref[l] = value[0, :4]
         cr_ref[l] = value[1, :4]
-        factors = f_ref[l]
-        low = low_half(factors.shape)
+
+    def update(l):
         for h in range(2):
-            kept = jnp.where(low == (h == 0), factors, jnp.zeros_like(factors))
             rows = pl.ds(half * h, half)
-            w[l, rows] = (w[l, rows].astype(F32) - STEP * dot(p_ref[l], kept, TN)).astype(BF16)
-
-    def each(function):
-        lax.fori_loop(0, layers, lambda l, carry: (function(l, None), carry)[1], 0)
+            w[l, rows] = updated(w[l, rows], p_ref[l], f_ref[l], h)
+
+    def turn(l):
+        for j in range(depth // 256):
+            wt[l, :, 256 * j:256 * (j + 1)] = w[l, 256 * j:256 * (j + 1)].T
+
+    def each(function, count=layers):
+        lax.fori_loop(0, count, lambda l, carry: (function(l, None), carry)[1], 0)
 
     for e in range(2):
         warm_load(e).wait()
@@ -227,6 +245,7 @@
     for e in range(2):
         warm_copy(e).start()
     each(own_edges)
+
     for e in range(2):
         warm_copy(e).wait_recv()
     each(other_edges)
@@ -235,7 +254,8 @@
     each(second_forward)
     each(lambda l, _: add_up(1, l, 0, 4))
     each(lambda l, _: backward(1, l))
-    each(last)
+    each(lambda l, _: (last(l, None), update(l)), layers - 1)
+    last(layers - 1, None)
     for e in range(2):
         warm_copy(e).wait_send()
 
@@ -260,14 +280,15 @@
         exchange_kernel,
         out_shape=(
             jax.ShapeDtypeStruct((layers, depth, width), BF16),
+            jax.ShapeDtypeStruct((layers, 64, half), BF16),
+            jax.ShapeDtypeStruct((layers, 64, width), BF16),
             jax.ShapeDtypeStruct((layers, 4, width), F32),
             jax.ShapeDtypeStruct((layers, 4, width), F32),
         ),
         in_specs=[hbm] * 3,
-        out_specs=(vmem,) * 3,
+        out_specs=(vmem,) * 5,
         scratch_shapes=[
-            pltpu.VMEM((layers, 64, half), BF16),
-            pltpu.VMEM((layers, 64, width), BF16),
+            pltpu.VMEM((layers, width, depth), BF16),
             pltpu.VMEM((4, layers, 4, width), BF16),
             pltpu.VMEM((layers, 4, 8, half), F32),
             pltpu.VMEM((2, layers, 4, 8, half), BF16),
@@ -281,25 +302,31 @@
             dma((2, layers, 2)), dma((2, layers, 2)),
             dma((2, layers)), dma((2, layers)), dma((2, layers)), dma((2, layers)),
         ],
-        compiler_params=pltpu.CompilerParams(collective_id=0, has_side_effects=True, vmem_limit_bytes=20 * 2**20),
+        compiler_params=pltpu.CompilerParams(collective_id=0, has_side_effects=True, vmem_limit_bytes=36 * 2**20),
         name="exchange",
     )(weights, warm_down, warm_right)
 
 
-def write_kernel(w_ref, down_ref, right_ref, w_out, down_out, right_out, sems):
-    layers = w_ref.shape[0]
-    copies = [
-        pltpu.make_async_copy(down_ref, down_out.at[0, 0], sems.at[0]),
-        pltpu.make_async_copy(right_ref, right_out.at[0, 0], sems.at[1]),
+def write_kernel(w_ref, p_ref, f_ref, down_ref, right_ref, w_out, down_out, right_out, rest, sems):
+    layers, depth, _ = w_ref.shape
+    half, l = depth // 2, layers - 1
+    copies = [pltpu.make_async_copy(w_ref.at[i], w_out.at[0, 0, i], sems.at[i]) for i in range(l)]
+    copies += [
+        pltpu.make_async_copy(down_ref, down_out.at[0, 0], sems.at[l + 2]),
+        pltpu.make_async_copy(right_ref, right_out.at[0, 0], sems.at[l + 3]),
     ]
-    copies += [pltpu.make_async_copy(w_ref.at[l], w_out.at[0, 0, l], sems.at[2 + l]) for l in range(layers)]
     for copy in copies:
         copy.start()
+    for h in range(2):
+        rows = pl.ds(half * h, half)
+        rest[rows] = updated(w_ref[l, rows], p_ref[l], f_ref[l], h)
+        copies.append(pltpu.make_async_copy(rest.at[rows], w_out.at[0, 0, l, rows], sems.at[l + h]))
+        copies[-1].start()
     for copy in copies:
         copy.wait()
 
 
-def write(w, down, right):
+def write(w, basis, factors, down, right):
     layers, depth, width = w.shape
     vmem = pl.BlockSpec(memory_space=pltpu.VMEM)
     hbm = pl.BlockSpec(memory_space=pltpu.HBM)
@@ -310,12 +337,12 @@
             jax.ShapeDtypeStruct((1, 1, layers, 4, width), F32),
             jax.ShapeDtypeStruct((1, 1, layers, 4, width), F32),
         ),
-        in_specs=[vmem] * 3,
+        in_specs=[vmem] * 5,
         out_specs=(hbm,) * 3,
-        scratch_shapes=[pltpu.SemaphoreType.DMA((2 + layers,))],
-        compiler_params=pltpu.CompilerParams(vmem_limit_bytes=2**20),
+        scratch_shapes=[pltpu.VMEM((depth, width), BF16), pltpu.SemaphoreType.DMA((layers + 3,))],
+        compiler_params=pltpu.CompilerParams(vmem_limit_bytes=8 * 2**20),
         name="write",
-    )(w, down, right)
+    )(w, basis, factors, down, right)
 
 
 def body(weights, warm_down, warm_right):

time: 51.5 us -> 49.3 us (0.957)
  Pallas kernels: 50.8 us -> 48.6 us
    pallas_call x1, Pallas kernels: 46.3 us -> 44.1 us  [exchange(): pl.pallas_call(exchange_kernel, out_shape=(jax.ShapeDtypeStruct((layers,...]
where the time goes in v3:
time: 49.3 us; the launch traced here: 49.2 us
  Pallas kernels  48.6 us (99%)
  between operations  0.64 us (1%)
    pallas_call x1, Pallas kernels, exchange(): pl.pallas_call(exchange_kernel, out_shape=(jax.ShapeDtypeStruct((layers,...  44.1 us
    pallas_call x1, Pallas kernels, write(): pl.pallas_call(write_kernel, out_shape=(jax.ShapeDtypeStruct((1, 1, layer...  4.44 us

profile of v3, /device:TPU:1, one launch (start us, length us, event | category | flops | bytes accessed | tf_op | source)
XLA Modules:
  0.0 49.2 jit_solution(8741435854147925495)
XLA Ops:
  0.6 44.1 %exchange.1 = (bf16[5,2304,512]{2,1,0:T(8,128)(2,1)S(1)}, bf16[5,64,1152]{2,1,0:T(8,128)(2,1)S(1)}, bf16[5,64,512]{2,1,0:T(8,128)(2,1)S(1)}, f32[5,4,512]{2,1,0:T(4,128)S(1)}, f32[5,4,512]{2,1,0:T(4,128)S(1)}) custom-call(bf16[1,1,5,2304,512]{4,3,2,1,0:T(8,128)(2,1)} %w_hbm.1, bf16[1,1,5,4,512]{4,3,2,1,0:T(4,128)(2,1)} %wd_hbm.1, ...), custom_call_target="tpu_custom_call" | custom-call | tf_op jit(solution)/shard_map/exchange/pallas_call | solution.py:279
  44.8 4.4 %write.1 = (bf16[1,1,5,2304,512]{4,3,2,1,0:T(8,128)(2,1)}, f32[1,1,5,4,512]{4,3,2,1,0:T(4,128)}, f32[1,1,5,4,512]{4,3,2,1,0:T(4,128)}) custom-call(bf16[5,2304,512]{2,1,0:T(8,128)(2,1)S(1)} %get-tuple-element.8.w_ref, bf16[5,64,1152]{2,1,0:T(8,128)(2,1)S(1)} %get-tuple-element.9.p_ref, bf16[5,64,512]{2,1,0:T(8,128)(2,1)S(1)} %get-tuple-element.10.f_ref, ...), custom_call_target="tpu_custom_call" | custom-call | tf_op jit(solution)/shard_map/write/pallas_call | solution.py:333

commit v4 on v3

--- a/solution.py
+++ b/solution.py
@@ -136,21 +136,21 @@
         return pltpu.make_async_remote_copy(
             send3.at[r, l], recv3.at[r, l], s3.at[r, l], r3.at[r, l], device_id=partner, device_id_type=MESH)
 
-    def forward(factors, l, turned=True):
-        if turned:
-            first = dot(factors, wt[l, :, :half], NN)
-            second = dot(factors, wt[l, :, half:], NN)
-        else:
-            first = dot(factors, w[l, :half], NT)
-            second = dot(factors, w[l, half:], NT)
+    def forward(factors, l, turned):
+        first = dot(factors, wt[l, :, :half], NN) if turned else dot(factors, w[l, :half], NT)
+        second = dot(factors, wt[l, :, half:], NN) if turned else dot(factors, w[l, half:], NT)
         return jnp.where(low_half(first.shape), first, second)
+
+    def masked(overlap):
+        same = low_half(overlap.shape) == (lax.broadcasted_iota(jnp.int32, overlap.shape, 1) % 8 < 4)
+        return jnp.where(same, overlap, 0.0).astype(BF16)
 
     def first_forward(l, e):
         pieces = []
         for i in (e, e + 1):
             rows = warm[i, l].astype(F32)
             pieces += [rows, rows]
-        product = forward(jnp.concatenate(pieces, axis=0).astype(BF16), l, False)
+        product = forward(jnp.concatenate(pieces, axis=0).astype(BF16), l, e > 0)
         product = product.reshape(2, 8, half)
         total[l, e:e + 2] = product
         send1[0, l, e:e + 2] = product.astype(BF16)
@@ -163,6 +163,8 @@
         def _():
             w_load(l + 2).start()
 
+        for j in range(depth // 256):
+            wt[l, :, 256 * j:256 * (j + 1)] = w[l, 256 * j:256 * (j + 1)].T
         first_forward(l, 0)
 
     def other_edges(l, _):
@@ -188,14 +190,15 @@
         for j, piece in enumerate(orthonormal(mine, theirs, chunks)):
             p_ref[l, 32 * r:32 * (r + 1), 128 * j:128 * (j + 1)] = piece.reshape(32, 128).astype(BF16)
         basis = p_ref[l, 32 * r:32 * (r + 1)]
+        if r:
+            overlap = masked(dot(basis, p_ref[l, :32], NT))
         first = dot(basis, w[l, :half], NN)
+        if r:
+            correction = STEP * dot(overlap, f_ref[l, :32], NN)
         second = dot(basis, w[l, half:], NN)
         parts = jnp.where(low_half(first.shape), first, second)
         if r:
-            overlap = dot(basis, p_ref[l, :32], NT)
-            same = low_half(overlap.shape) == (lax.broadcasted_iota(jnp.int32, overlap.shape, 1) % 8 < 4)
-            overlap = jnp.where(same, overlap, 0.0).astype(BF16)
-            parts = parts - STEP * dot(overlap, f_ref[l, :32], NN)
+            parts = parts - correction
         parts = parts.reshape(4, 8, width)
         value = parts + pltpu.roll(parts, 4, 1)
         back[l] = value
@@ -212,11 +215,11 @@
 
     def second_forward(l, _):
         _, factors = combine(0, l)
-        product = forward(factors, l, False)
-        overlap = dot(factors, factors, NT)
-        same = low_half(overlap.shape) == (lax.broadcasted_iota(jnp.int32, overlap.shape, 1) % 8 < 4)
-        overlap = jnp.where(same, overlap, 0.0).astype(BF16)
-        product = product - STEP * dot(overlap, p_ref[l, :32], NN)
+        overlap = masked(dot(factors, factors, NT))
+        first = dot(factors, wt[l, :, :half], NN)
+        correction = STEP * dot(overlap, p_ref[l, :32], NN)
+        second = dot(factors, wt[l, :, half:], NN)
+        product = jnp.where(low_half(first.shape), first, second) - correction
         product = product.reshape(4, 8, half)
         total[l] = product
         send1[1, l] = product.astype(BF16)
@@ -231,10 +234,6 @@
         for h in range(2):
             rows = pl.ds(half * h, half)
             w[l, rows] = updated(w[l, rows], p_ref[l], f_ref[l], h)
-
-    def turn(l):
-        for j in range(depth // 256):
-            wt[l, :, 256 * j:256 * (j + 1)] = w[l, 256 * j:256 * (j + 1)].T
 
     def each(function, count=layers):
         lax.fori_loop(0, count, lambda l, carry: (function(l, None), carry)[1], 0)
@@ -254,8 +253,6 @@
     each(second_forward)
     each(lambda l, _: add_up(1, l, 0, 4))
     each(lambda l, _: backward(1, l))
-    each(lambda l, _: (last(l, None), update(l)), layers - 1)
-    last(layers - 1, None)
     for e in range(2):
         warm_copy(e).wait_send()
 
@@ -263,11 +260,20 @@
         mp_copy(0, l, 0, 2).wait_send()
         mp_copy(0, l, 2, 2).wait_send()
         mp_copy(1, l, 0, 4).wait_send()
-        for r in range(2):
-            sums_copy(r, l).wait_send()
-            backs_copy(r, l).wait_send()
+        sums_copy(0, l).wait_send()
+        sums_copy(1, l).wait_send()
+        backs_copy(0, l).wait_send()
 
     each(drain)
+
+    def finish(l, _):
+        last(l, None)
+        update(l)
+        backs_copy(1, l).wait_send()
+
+    each(finish, layers - 1)
+    last(layers - 1, None)
+    backs_copy(1, layers - 1).wait_send()
 
 
 def exchange(weights, warm_down, warm_right):
@@ -310,17 +316,20 @@
 def write_kernel(w_ref, p_ref, f_ref, down_ref, right_ref, w_out, down_out, right_out, rest, sems):
     layers, depth, _ = w_ref.shape
     half, l = depth // 2, layers - 1
-    copies = [pltpu.make_async_copy(w_ref.at[i], w_out.at[0, 0, i], sems.at[i]) for i in range(l)]
-    copies += [
-        pltpu.make_async_copy(down_ref, down_out.at[0, 0], sems.at[l + 2]),
-        pltpu.make_async_copy(right_ref, right_out.at[0, 0], sems.at[l + 3]),
+    copies = [
+        pltpu.make_async_copy(down_ref, down_out.at[0, 0], sems.at[l, 0]),
+        pltpu.make_async_copy(right_ref, right_out.at[0, 0], sems.at[l, 1]),
     ]
+    for i in range(l):
+        for h in range(2):
+            rows = pl.ds(half * h, half)
+            copies.append(pltpu.make_async_copy(w_ref.at[i, rows], w_out.at[0, 0, i, rows], sems.at[i, h]))
     for copy in copies:
         copy.start()
     for h in range(2):
         rows = pl.ds(half * h, half)
         rest[rows] = updated(w_ref[l, rows], p_ref[l], f_ref[l], h)
-        copies.append(pltpu.make_async_copy(rest.at[rows], w_out.at[0, 0, l, rows], sems.at[l + h]))
+        copies.append(pltpu.make_async_copy(rest.at[rows], w_out.at[0, 0, l, rows], sems.at[l + 1, h]))
         copies[-1].start()
     for copy in copies:
         copy.wait()
@@ -339,7 +348,7 @@
         ),
         in_specs=[vmem] * 5,
         out_specs=(hbm,) * 3,
-        scratch_shapes=[pltpu.VMEM((depth, width), BF16), pltpu.SemaphoreType.DMA((layers + 3,))],
+        scratch_shapes=[pltpu.VMEM((depth, width), BF16), pltpu.SemaphoreType.DMA((layers + 1, 2))],
         compiler_params=pltpu.CompilerParams(vmem_limit_bytes=8 * 2**20),
         name="write",
     )(w, basis, factors, down, right)

time: 49.3 us -> 48.5 us (0.984)
  Pallas kernels: 48.6 us -> 47.8 us
    pallas_call x1, Pallas kernels: 44.1 us -> 43.3 us  [exchange(): pl.pallas_call(exchange_kernel, out_shape=(jax.ShapeDtypeStruct((layers,...]
where the time goes in v4:
time: 48.5 us; the launch traced here: 48.4 us
  Pallas kernels  47.8 us (99%)
  between operations  0.64 us (1%)
    pallas_call x1, Pallas kernels, exchange(): pl.pallas_call(exchange_kernel, out_shape=(jax.ShapeDtypeStruct((layers,...  43.3 us
    pallas_call x1, Pallas kernels, write(): pl.pallas_call(write_kernel, out_shape=(jax.ShapeDtypeStruct((1, 1, layer...  4.48 us

profile of v4, /device:TPU:1, one launch (start us, length us, event | category | flops | bytes accessed | tf_op | source)
XLA Modules:
  0.0 48.4 jit_solution(10943910820433720334)
XLA Ops:
  0.6 43.3 %exchange.1 = (bf16[5,2304,512]{2,1,0:T(8,128)(2,1)S(1)}, bf16[5,64,1152]{2,1,0:T(8,128)(2,1)S(1)}, bf16[5,64,512]{2,1,0:T(8,128)(2,1)S(1)}, f32[5,4,512]{2,1,0:T(4,128)S(1)}, f32[5,4,512]{2,1,0:T(4,128)S(1)}) custom-call(bf16[1,1,5,2304,512]{4,3,2,1,0:T(8,128)(2,1)} %w_hbm.1, bf16[1,1,5,4,512]{4,3,2,1,0:T(4,128)(2,1)} %wd_hbm.1, ...), custom_call_target="tpu_custom_call" | custom-call | tf_op jit(solution)/shard_map/exchange/pallas_call | solution.py:285
  43.9 4.5 %write.1 = (bf16[1,1,5,2304,512]{4,3,2,1,0:T(8,128)(2,1)}, f32[1,1,5,4,512]{4,3,2,1,0:T(4,128)}, f32[1,1,5,4,512]{4,3,2,1,0:T(4,128)}) custom-call(bf16[5,2304,512]{2,1,0:T(8,128)(2,1)S(1)} %get-tuple-element.8.w_ref, bf16[5,64,1152]{2,1,0:T(8,128)(2,1)S(1)} %get-tuple-element.9.p_ref, bf16[5,64,512]{2,1,0:T(8,128)(2,1)S(1)} %get-tuple-element.10.f_ref, ...), custom_call_target="tpu_custom_call" | custom-call | tf_op jit(solution)/shard_map/write/pallas_call | solution.py:342

commit v5 on v4

--- a/solution.py
+++ b/solution.py
@@ -106,16 +106,16 @@
 
     for e in range(2):
         warm_load(e).start()
-    for l in range(2):
+    for l in range(3):
         w_load(l).start()
 
     def warm_copy(e):
         return pltpu.make_async_remote_copy(
             warm.at[e], warm.at[e + 2], warm_send.at[e], warm_recv.at[e], device_id=straight[e], device_id_type=MESH)
 
-    def mp_copy(r, l, e, n):
-        return pltpu.make_async_remote_copy(
-            send1.at[r, l, pl.ds(e, n)], recv1.at[r, l, pl.ds(e, n)], s1.at[r, l, e // 2], r1.at[r, l, e // 2],
+    def mp_copy(r, l, e):
+        return pltpu.make_async_remote_copy(
+            send1.at[r, l, e], recv1.at[r, l, e], s1.at[r, l, e], r1.at[r, l, e],
             device_id=partner, device_id_type=MESH)
 
     def sum_copy(r, l, e):
@@ -154,14 +154,15 @@
         product = product.reshape(2, 8, half)
         total[l, e:e + 2] = product
         send1[0, l, e:e + 2] = product.astype(BF16)
-        mp_copy(0, l, e, 2).start()
+        for i in (e, e + 1):
+            mp_copy(0, l, i).start()
 
     def own_edges(l, _):
         w_load(l).wait()
 
-        @pl.when(l + 2 < layers)
+        @pl.when(l + 3 < layers)
         def _():
-            w_load(l + 2).start()
+            w_load(l + 3).start()
 
         for j in range(depth // 256):
             wt[l, :, 256 * j:256 * (j + 1)] = w[l, 256 * j:256 * (j + 1)].T
@@ -170,13 +171,13 @@
     def other_edges(l, _):
         first_forward(l, 2)
 
-    def add_up(r, l, e, n):
-        mp_copy(r, l, e, n).wait_recv()
-        value = total[l, e:e + n] + recv1[r, l, e:e + n].astype(F32)
-        total[l, e:e + n] = value
-        send2[r, l, e:e + n] = value.astype(BF16)
-        for i in range(e, e + n):
-            sum_copy(r, l, i).start()
+    def add_up(r, l, slots):
+        for e in slots:
+            mp_copy(r, l, e).wait_recv()
+            value = total[l, e] + recv1[r, l, e].astype(F32)
+            total[l, e] = value
+            send2[r, l, e] = value.astype(BF16)
+            sum_copy(r, l, e).start()
 
     def backward(r, l):
         sums_copy(r, l).wait_recv()
@@ -203,7 +204,7 @@
         value = parts + pltpu.roll(parts, 4, 1)
         back[l] = value
         send3[r, l] = value.astype(BF16)
-        for e in range(4):
+        for e in (0, 2, 1, 3):
             back_copy(r, l, e).start()
 
     def combine(r, l):
@@ -223,7 +224,8 @@
         product = product.reshape(4, 8, half)
         total[l] = product
         send1[1, l] = product.astype(BF16)
-        mp_copy(1, l, 0, 4).start()
+        for e in (0, 2, 1, 3):
+            mp_copy(1, l, e).start()
 
     def last(l, _):
         value, _ = combine(1, l)
@@ -248,18 +250,18 @@
     for e in range(2):
         warm_copy(e).wait_recv()
     each(other_edges)
-    each(lambda l, _: (add_up(0, l, 0, 2), add_up(0, l, 2, 2)))
+    each(lambda l, _: add_up(0, l, (0, 1, 2, 3)))
     each(lambda l, _: backward(0, l))
     each(second_forward)
-    each(lambda l, _: add_up(1, l, 0, 4))
+    each(lambda l, _: add_up(1, l, (0, 2, 1, 3)))
     each(lambda l, _: backward(1, l))
     for e in range(2):
         warm_copy(e).wait_send()
 
     def drain(l, _):
-        mp_copy(0, l, 0, 2).wait_send()
-        mp_copy(0, l, 2, 2).wait_send()
-        mp_copy(1, l, 0, 4).wait_send()
+        for r in range(2):
+            for e in range(4):
+                mp_copy(r, l, e).wait_send()
         sums_copy(0, l).wait_send()
         sums_copy(1, l).wait_send()
         backs_copy(0, l).wait_send()
@@ -305,7 +307,7 @@
             pltpu.VMEM((2, layers, 4, 8, width), BF16),
             pltpu.VMEM((2, layers, 4, 8, width), BF16),
             dma((layers,)), dma((2,)), dma((2,)), dma((2,)),
-            dma((2, layers, 2)), dma((2, layers, 2)),
+            dma((2, layers, 4)), dma((2, layers, 4)),
             dma((2, layers)), dma((2, layers)), dma((2, layers)), dma((2, layers)),
         ],
         compiler_params=pltpu.CompilerParams(collective_id=0, has_side_effects=True, vmem_limit_bytes=36 * 2**20),

time: 48.5 us -> 48.2 us (level)
  no operation moved by 1% of the time
where the time goes in v5:
time: 48.2 us; the launch traced here: 48.1 us
  Pallas kernels  47.5 us (99%)
  between operations  0.64 us (1%)
    pallas_call x1, Pallas kernels, exchange(): pl.pallas_call(exchange_kernel, out_shape=(jax.ShapeDtypeStruct((layers,...  43 us
    pallas_call x1, Pallas kernels, write(): pl.pallas_call(write_kernel, out_shape=(jax.ShapeDtypeStruct((1, 1, layer...  4.48 us

profile of v5, /device:TPU:1, one launch (start us, length us, event | category | flops | bytes accessed | tf_op | source)
XLA Modules:
  0.0 48.1 jit_solution(6517798242605924418)
XLA Ops:
  0.6 43.0 %exchange.1 = (bf16[5,2304,512]{2,1,0:T(8,128)(2,1)S(1)}, bf16[5,64,1152]{2,1,0:T(8,128)(2,1)S(1)}, bf16[5,64,512]{2,1,0:T(8,128)(2,1)S(1)}, f32[5,4,512]{2,1,0:T(4,128)S(1)}, f32[5,4,512]{2,1,0:T(4,128)S(1)}) custom-call(bf16[1,1,5,2304,512]{4,3,2,1,0:T(8,128)(2,1)} %w_hbm.1, bf16[1,1,5,4,512]{4,3,2,1,0:T(4,128)(2,1)} %wd_hbm.1, ...), custom_call_target="tpu_custom_call" | custom-call | tf_op jit(solution)/shard_map/exchange/pallas_call | solution.py:287
  43.6 4.5 %write.1 = (bf16[1,1,5,2304,512]{4,3,2,1,0:T(8,128)(2,1)}, f32[1,1,5,4,512]{4,3,2,1,0:T(4,128)}, f32[1,1,5,4,512]{4,3,2,1,0:T(4,128)}) custom-call(bf16[5,2304,512]{2,1,0:T(8,128)(2,1)S(1)} %get-tuple-element.8.w_ref, bf16[5,64,1152]{2,1,0:T(8,128)(2,1)S(1)} %get-tuple-element.9.p_ref, bf16[5,64,512]{2,1,0:T(8,128)(2,1)S(1)} %get-tuple-element.10.f_ref, ...), custom_call_target="tpu_custom_call" | custom-call | tf_op jit(solution)/shard_map/write/pallas_call | solution.py:344

commit v6 on v5

--- a/solution.py
+++ b/solution.py
@@ -273,9 +273,10 @@
         update(l)
         backs_copy(1, l).wait_send()
 
-    each(finish, layers - 1)
-    last(layers - 1, None)
-    backs_copy(1, layers - 1).wait_send()
+    each(finish, layers - 2)
+    for l in (layers - 2, layers - 1):
+        last(l, None)
+        backs_copy(1, l).wait_send()
 
 
 def exchange(weights, warm_down, warm_right):
@@ -317,22 +318,23 @@
 
 def write_kernel(w_ref, p_ref, f_ref, down_ref, right_ref, w_out, down_out, right_out, rest, sems):
     layers, depth, _ = w_ref.shape
-    half, l = depth // 2, layers - 1
+    half, kept = depth // 2, layers - 2
     copies = [
-        pltpu.make_async_copy(down_ref, down_out.at[0, 0], sems.at[l, 0]),
-        pltpu.make_async_copy(right_ref, right_out.at[0, 0], sems.at[l, 1]),
+        pltpu.make_async_copy(down_ref, down_out.at[0, 0], sems.at[layers, 0]),
+        pltpu.make_async_copy(right_ref, right_out.at[0, 0], sems.at[layers, 1]),
     ]
-    for i in range(l):
+    for l in range(kept):
         for h in range(2):
             rows = pl.ds(half * h, half)
-            copies.append(pltpu.make_async_copy(w_ref.at[i, rows], w_out.at[0, 0, i, rows], sems.at[i, h]))
+            copies.append(pltpu.make_async_copy(w_ref.at[l, rows], w_out.at[0, 0, l, rows], sems.at[l, h]))
     for copy in copies:
         copy.start()
-    for h in range(2):
-        rows = pl.ds(half * h, half)
-        rest[rows] = updated(w_ref[l, rows], p_ref[l], f_ref[l], h)
-        copies.append(pltpu.make_async_copy(rest.at[rows], w_out.at[0, 0, l, rows], sems.at[l + 1, h]))
-        copies[-1].start()
+    for l in range(kept, layers):
+        for h in range(2):
+            rows = pl.ds(half * h, half)
+            rest[l - kept, rows] = updated(w_ref[l, rows], p_ref[l], f_ref[l], h)
+            copies.append(pltpu.make_async_copy(rest.at[l - kept, rows], w_out.at[0, 0, l, rows], sems.at[l, h]))
+            copies[-1].start()
     for copy in copies:
         copy.wait()
 
@@ -350,8 +352,8 @@
         ),
         in_specs=[vmem] * 5,
         out_specs=(hbm,) * 3,
-        scratch_shapes=[pltpu.VMEM((depth, width), BF16), pltpu.SemaphoreType.DMA((layers + 1, 2))],
-        compiler_params=pltpu.CompilerParams(vmem_limit_bytes=8 * 2**20),
+        scratch_shapes=[pltpu.VMEM((2, depth, width), BF16), pltpu.SemaphoreType.DMA((layers + 1, 2))],
+        compiler_params=pltpu.CompilerParams(vmem_limit_bytes=10 * 2**20),
         name="write",
     )(w, basis, factors, down, right)
 

time: 48.2 us -> 48.2 us (level)
  no operation moved by 1% of the time
where the time goes in v6:
time: 48.2 us; the launch traced here: 48.1 us
  Pallas kernels  47.5 us (99%)
  between operations  0.64 us (1%)
    pallas_call x1, Pallas kernels, exchange(): pl.pallas_call(exchange_kernel, out_shape=(jax.ShapeDtypeStruct((layers,...  43 us
    pallas_call x1, Pallas kernels, write(): pl.pallas_call(write_kernel, out_shape=(jax.ShapeDtypeStruct((1, 1, layer...  4.48 us

profile of v6, /device:TPU:1, one launch (start us, length us, event | category | flops | bytes accessed | tf_op | source)
XLA Modules:
  0.0 48.1 jit_solution(14568001262598428475)
XLA Ops:
  0.6 43.0 %exchange.1 = (bf16[5,2304,512]{2,1,0:T(8,128)(2,1)S(1)}, bf16[5,64,1152]{2,1,0:T(8,128)(2,1)S(1)}, bf16[5,64,512]{2,1,0:T(8,128)(2,1)S(1)}, f32[5,4,512]{2,1,0:T(4,128)S(1)}, f32[5,4,512]{2,1,0:T(4,128)S(1)}) custom-call(bf16[1,1,5,2304,512]{4,3,2,1,0:T(8,128)(2,1)} %w_hbm.1, bf16[1,1,5,4,512]{4,3,2,1,0:T(4,128)(2,1)} %wd_hbm.1, ...), custom_call_target="tpu_custom_call" | custom-call | tf_op jit(solution)/shard_map/exchange/pallas_call | solution.py:288
  43.6 4.5 %write.1 = (bf16[1,1,5,2304,512]{4,3,2,1,0:T(8,128)(2,1)}, f32[1,1,5,4,512]{4,3,2,1,0:T(4,128)}, f32[1,1,5,4,512]{4,3,2,1,0:T(4,128)}) custom-call(bf16[5,2304,512]{2,1,0:T(8,128)(2,1)S(1)} %get-tuple-element.8.w_ref, bf16[5,64,1152]{2,1,0:T(8,128)(2,1)S(1)} %get-tuple-element.9.p_ref, bf16[5,64,512]{2,1,0:T(8,128)(2,1)S(1)} %get-tuple-element.10.f_ref, ...), custom_call_target="tpu_custom_call" | custom-call | tf_op jit(solution)/shard_map/write/pallas_call | solution.py:346
